TPU v7x, 32 devices: a whole 2x2x4 slice. The times are simulated.
32 devices in a mesh: gx: 4 (over y, x), gy: 2 (over core), gz: 4 (over z).
Axes of the slice: x: 2, y: 2, z: 4, core: 2. Of those that a mesh axis runs over, the one named last changes fastest.
Arguments:
- measures: float32 [65536, 256], P(('gx', 'gy', 'gz')), may hold values from -6 to 6
- group_index: int32 [65536], P(('gx', 'gy', 'gz')), may hold values from 0 to 511, as said below
- distinct_keys: int32 [32, 512], P(('gx', 'gy', 'gz')), may hold values from 32 to 65567, as said below
- group_counts: int32 [32], P(('gx', 'gy', 'gz')), may hold values from 128 to 512, as said below
Outputs:
- group_sums: float32 [16384, 256], P(('gx', 'gy', 'gz'))
- group_rows: int32 [16384], P(('gx', 'gy', 'gz'))
- group_keys: int32 [16384], P(('gx', 'gy', 'gz'))
- group_total: int32 [], replicated
Inputs may be any that keep to these rules, and one draw needn't show every extreme that they name: `group_counts`: every device has between 128 and 512 groups, and some device has exactly 512. `group_index`: each row's index lies below its device's group count, and every group of a device has at least one row. `distinct_keys`: each device's keys rise strictly; all keys of device d equal d modulo 32, so no key lives on two devices; entries at and past the device's count are unused.
All inputs are finite; a program needn't handle non-finite values.
Results may differ from a plain program's by a relative error of at most 0.0003.
Values sent between devices are 32-bit elements; how exact they have to be, the bound alone decides.
A program may use at most 64 MiB of HBM per device.

v0:
```python
import jax
import jax.numpy as jnp
from jax import lax
from jax.sharding import PartitionSpec as P


def shards(measures, group_index, distinct_keys, group_counts):
    rows, width = measures.shape
    span = distinct_keys.shape[1]
    devices = lax.axis_size(("gx", "gy", "gz"))
    slots = span // devices
    plane = lax.axis_size("gx") * lax.axis_size("gy")
    line = lax.axis_size("gz")
    count = group_counts[0]
    myself = jnp.int32(0)
    sender_counts = lax.all_gather(group_counts, ("gx", "gy", "gz"), axis=0, tiled=True)
    sender_offsets = jnp.cumsum(sender_counts) - sender_counts
    myself = lax.axis_index(("gx", "gy", "gz"))
    offset = sender_offsets[myself]
    group_total = jnp.sum(sender_counts)
    block = min(1024, rows)
    labels = lax.broadcasted_iota(jnp.int32, (span, block), 0)

    def accumulate(step, carry):
        totals, tallies = carry
        start = step * block
        index = lax.dynamic_slice_in_dim(group_index, start, block)
        values = lax.dynamic_slice_in_dim(measures, start, block, 0)
        hits = index[None, :] == labels
        totals = totals + jnp.dot(
            hits.astype(jnp.float32),
            values,
            precision=lax.Precision.HIGHEST,
            preferred_element_type=jnp.float32,
        )
        tallies = tallies + jnp.sum(hits, axis=1, dtype=jnp.int32)
        return (totals, tallies)

    sums, tallies = lax.fori_loop(
        0,
        rows // block,
        accumulate,
        (jnp.zeros((span, width), jnp.float32), jnp.zeros((span,), jnp.int32)),
    )
    local = jnp.arange(span, dtype=jnp.int32)
    live = local < count
    keys = jnp.where(live, distinct_keys[0], -1)
    fields = jnp.stack([tallies.astype(jnp.float32), keys.astype(jnp.float32)], axis=1)
    extra = fields.shape[1]

    def arrange(array):
        shaped = array.reshape((slots, devices) + array.shape[1:])
        rolled = jnp.roll(shaped, offset, axis=1)
        return rolled.reshape((slots, plane, line) + array.shape[1:])

    outgoing = (arrange(sums), arrange(fields))
    arrived = (
        lax.all_to_all(
            lax.all_to_all(outgoing[0], "gz", split_axis=2, concat_axis=2, tiled=True),
            ("gx", "gy"),
            split_axis=1,
            concat_axis=1,
            tiled=True,
        ),
        lax.all_to_all(
            lax.all_to_all(outgoing[1], "gz", split_axis=2, concat_axis=2, tiled=True),
            ("gx", "gy"),
            split_axis=1,
            concat_axis=1,
            tiled=True,
        ),
    )
    got_sums, got_fields = arrived
    got_fields = got_fields.reshape(-1, extra)
    sender = jnp.arange(devices, dtype=jnp.int32).reshape(1, plane, line)
    start_of = sender_offsets.reshape(1, plane, line)
    count_of = sender_counts.reshape(1, plane, line)
    level = jnp.arange(slots, dtype=jnp.int32).reshape(slots, 1, 1)
    position = level * devices + (myself - start_of) % devices
    arrived_live = (position < count_of) & (sender >= 0)
    target = jnp.where(arrived_live, (start_of + position) // devices, span).reshape(-1)
    group_sums = (
        jnp.zeros((span, width), jnp.float32)
        .at[target]
        .set(got_sums.reshape(-1, width), mode="drop")
    )
    group_rows = (
        jnp.zeros((span,), jnp.int32)
        .at[target]
        .set(got_fields[:, 0].astype(jnp.int32), mode="drop")
    )
    group_keys = (
        jnp.full((span,), -1, jnp.int32)
        .at[target]
        .set(got_fields[:, 1].astype(jnp.int32), mode="drop")
    )
    return (group_sums, group_rows, group_keys, group_total)


def solution(mesh):
    return jax.shard_map(
        shards,
        mesh=mesh,
        in_specs=(
            P(("gx", "gy", "gz"), None),
            P(("gx", "gy", "gz")),
            P(("gx", "gy", "gz"), None),
            P(("gx", "gy", "gz")),
        ),
        out_specs=(P(("gx", "gy", "gz"), None), P(("gx", "gy", "gz")), P(("gx", "gy", "gz")), P()),
        check_vma=False,
    )
```

profile of v0, /device:TPU:0, one launch (start us, length us, event | category | flops | bytes accessed | tf_op | source)
XLA Modules:
  0.0 106.3 jit_solution(15189355763401430567)
XLA Ops:
  1.4 42.0 %all-reduce = s32[32]{0:T(128)S(1)} all-reduce(s32[32]{0:T(128)S(1)} %dynamic-update-slice), channel_id=1, replica_groups=mesh['gx'=4,'gy'=2,'gz'=4] {'gx','gy','gz'}, use_global_device_ids=true, to_apply=%add | all-reduce | flops 32 | bytes 256
  43.6 0.6 fusion.19
  44.3 0.6 dynamic_slice.25
  46.8 7.4 %while.16 = (s32[]{:T(128)}, f32[512,256]{1,0:T(8,128)S(1)}, s32[512]{0:T(512)S(1)}, s32[2048]{0:T(1024)}, f32[2048,256]{1,0:T(8,128)}, /*index=5*/s32[]{:T(128)}, s32[]{:T(128)}, s32[]{:T(128)}, s32[]{:T(128)}) while((s32[]{:T(128)}, f32[512,256]{1,0:T(8,128)S(1)}, s32[512]{0:T(512)S(1)}, s32[2048]{0:T(1024)}, ...), condition=%wide.region_3.4_spmd.clone, body=%wide.region_1.3_spmd.clone.sunk | while | flops 1612972544 | bytes 2121886 | solution.py:39
  46.9 0.7 dynamic_slice.55
  47.6 2.7 %fusion.24 = f32[512,256]{1,0:T(8,128)S(1)} fusion(f32[2048,256]{1,0:T(8,128)} %get-tuple-element.203, s32[]{:T(128)S(6)} %select_n.107, s32[1024]{0:T(1024)S(1)} %dynamic_slice.55, f32[512,256]{1,0:T(8,128)S(1)} %get-tuple-element.191, pred[]{:T(512)S(6)} %compare.20), kind=kOutput, calls=%fused_computation.8.clone.1 | convolution fusion | flops 1611399168 | bytes 2101253 | tf_op jit(solution)/shard_map/while/body/eval_jaxpr/dot_general | solution.py:30
  50.2 0.3 fusion.25
  50.6 0.7 dynamic_slice.55
  51.2 2.7 %fusion.24 = f32[512,256]{1,0:T(8,128)S(1)} fusion(f32[2048,256]{1,0:T(8,128)} %get-tuple-element.203, s32[]{:T(128)S(6)} %select_n.107, s32[1024]{0:T(1024)S(1)} %dynamic_slice.55, f32[512,256]{1,0:T(8,128)S(1)} %get-tuple-element.191, pred[]{:T(512)S(6)} %compare.20), kind=kOutput, calls=%fused_computation.8.clone.1 | convolution fusion | flops 1611399168 | bytes 2101253 | tf_op jit(solution)/shard_map/while/body/eval_jaxpr/dot_general | solution.py:30
  53.9 0.3 fusion.25
  54.3 0.5 broadcast.199
  54.8 0.7 reduce.5
  55.8 0.7 reshape.312
  56.5 3.6 %all-to-all-start.2 = ((f32[4,1,256]{2,1,0:T(1,128)}), f32[4,1,256]{2,1,0:T(1,128)S(1)}, u32[]{:S(2)}, u32[]{:S(2)}) async-start(f32[4,1,256]{2,1,0:T(1,128)} %reshape.312), calls=%async_computation.2 | async-start | bytes 8192 | tf_op jit(solution)/shard_map/all_to_all | solution.py:66
  60.2 0.3 copy.38
  60.5 1.1 %copy.39 = f32[16,8,4,256]{3,1,0,2:T(8,128)} copy(f32[16,8,4,256]{3,0,2,1:T(8,128)S(1)} %bitcast.23) | data formatting | bytes 1048576 | tf_op jit(solution)/shard_map/reshape | solution.py:54
  61.6 4.0 %all-to-all-done.2 = f32[4,1,256]{2,1,0:T(1,128)S(1)} async-done(((f32[4,1,256]{2,1,0:T(1,128)}), f32[4,1,256]{2,1,0:T(1,128)S(1)}, u32[]{:S(2)}, u32[]{:S(2)}) %all-to-all-start.2) | async-done | bytes 4128 | tf_op jit(solution)/shard_map/all_to_all | solution.py:66
  65.6 3.5 %all-to-all-start = ((f32[16,8,4,256]{3,1,0,2:T(8,128)}), f32[16,8,4,256]{3,1,0,2:T(8,128)S(1)}, u32[]{:S(2)}, u32[]{:S(2)}) async-start(f32[16,8,4,256]{3,1,0,2:T(8,128)} %copy.39), calls=%async_computation | async-start | bytes 1048576 | tf_op jit(solution)/shard_map/all_to_all | solution.py:59
  69.3 0.5 broadcast.200
  69.8 0.7 reduce.6
  70.6 0.7 reshape.314
  71.3 10.3 %all-to-all-done = f32[16,8,4,256]{3,1,0,2:T(8,128)S(1)} async-done(((f32[16,8,4,256]{3,1,0,2:T(8,128)}), f32[16,8,4,256]{3,1,0,2:T(8,128)S(1)}, u32[]{:S(2)}, u32[]{:S(2)}) %all-to-all-start) | async-done | bytes 524320 | tf_op jit(solution)/shard_map/all_to_all | solution.py:59
  81.6 3.6 %all-to-all-start.3 = ((f32[8,1,128]{2,1,0:T(1,128)}), f32[8,1,128]{2,1,0:T(1,128)S(1)}, u32[]{:S(2)}, u32[]{:S(2)}) async-start(f32[8,1,128]{2,1,0:T(1,128)} %reshape.314), calls=%async_computation.3 | async-start | bytes 8192 | tf_op jit(solution)/shard_map/all_to_all | solution.py:65
  85.2 1.1 %copy.40 = f32[16,8,4,256]{3,2,0,1:T(4,128)} copy(f32[16,8,4,256]{3,1,0,2:T(8,128)S(1)} %all-to-all-done) | data formatting | bytes 1048576 | tf_op jit(solution)/shard_map/all_to_all | solution.py:59
  86.4 3.5 %all-to-all-done.3 = f32[8,1,128]{2,1,0:T(1,128)S(1)} async-done(((f32[8,1,128]{2,1,0:T(1,128)}), f32[8,1,128]{2,1,0:T(1,128)S(1)}, u32[]{:S(2)}, u32[]{:S(2)}) %all-to-all-start.3) | async-done | bytes 4128 | tf_op jit(solution)/shard_map/all_to_all | solution.py:65
  89.8 3.5 %all-to-all-start.1 = ((f32[16,8,4,256]{3,2,0,1:T(4,128)}), f32[16,8,4,256]{3,2,0,1:T(4,128)S(1)}, u32[]{:S(2)}, u32[]{:S(2)}) async-start(f32[16,8,4,256]{3,2,0,1:T(4,128)} %copy.40), calls=%async_computation.1 | async-start | bytes 1048576 | tf_op jit(solution)/shard_map/all_to_all | solution.py:58
  93.7 0.7 reduce.7
  94.8 3.0 %scatter_custom_fusion.1 = s32[512]{0:T(512)} fusion(s32[512]{0:T(512)S(1)} %bitcast.30, s32[512]{0:T(512)S(1)} %bitcast.34, s32[]{:T(128)} %constant.107.clone.1), kind=kCustom, calls=%fused_computation.40 | custom fusion | bytes 2052 | tf_op jit(solution)/shard_map/scatter | solution.py:90
  97.8 3.0 %scatter_custom_fusion.2 = s32[512]{0:T(512)} fusion(s32[512]{0:T(512)S(1)} %bitcast.31, s32[512]{0:T(512)S(1)} %bitcast.33, s32[]{:T(128)} %constant.111.clone.1), kind=kCustom, calls=%fused_computation.38 | custom fusion | bytes 2052 | tf_op jit(solution)/shard_map/scatter | solution.py:95
  100.8 2.2 %all-to-all-done.1 = f32[16,8,4,256]{3,2,0,1:T(4,128)S(1)} async-done(((f32[16,8,4,256]{3,2,0,1:T(4,128)}), f32[16,8,4,256]{3,2,0,1:T(4,128)S(1)}, u32[]{:S(2)}, u32[]{:S(2)}) %all-to-all-start.1) | async-done | bytes 524320 | tf_op jit(solution)/shard_map/all_to_all | solution.py:58
  103.0 0.2 reshape.271
  103.2 3.0 %scatter_custom_fusion = f32[512,256]{1,0:T(8,128)} fusion(s32[512]{0:T(512)S(1)} %bitcast.32, f32[512,256]{1,0:T(8,128)S(1)} %reshape.271, f32[]{:T(128)} %constant.100.clone.1), kind=kCustom, calls=%fused_computation.16 | custom fusion | bytes 524292 | tf_op jit(solution)/shard_map/scatter | solution.py:85
  (36 shorter events, 2.0 us)
Async XLA Ops:
  46.8 8.0 %copy-start = (s32[1,512]{1,0:T(1,128)S(1)}, s32[1,512]{1,0:T(1,128)}, u32[]{:S(2)}) copy-start(s32[1,512]{1,0:T(1,128)} %param.8) | copy-start | bytes 6148
  56.5 9.2 %all-to-all-start.2 = ((f32[4,1,256]{2,1,0:T(1,128)}), f32[4,1,256]{2,1,0:T(1,128)S(1)}, u32[]{:S(2)}, u32[]{:S(2)}) async-start(f32[4,1,256]{2,1,0:T(1,128)} %reshape.312), calls=%async_computation.2 | async-start | bytes 8192 | tf_op jit(solution)/shard_map/all_to_all | solution.py:66
  65.6 16.0 %all-to-all-start = ((f32[16,8,4,256]{3,1,0,2:T(8,128)}), f32[16,8,4,256]{3,1,0,2:T(8,128)S(1)}, u32[]{:S(2)}, u32[]{:S(2)}) async-start(f32[16,8,4,256]{3,1,0,2:T(8,128)} %copy.39), calls=%async_computation | async-start | bytes 1048576 | tf_op jit(solution)/shard_map/all_to_all | solution.py:59
  81.6 8.2 %all-to-all-start.3 = ((f32[8,1,128]{2,1,0:T(1,128)}), f32[8,1,128]{2,1,0:T(1,128)S(1)}, u32[]{:S(2)}, u32[]{:S(2)}) async-start(f32[8,1,128]{2,1,0:T(1,128)} %reshape.314), calls=%async_computation.3 | async-start | bytes 8192 | tf_op jit(solution)/shard_map/all_to_all | solution.py:65
  89.8 13.2 %all-to-all-start.1 = ((f32[16,8,4,256]{3,2,0,1:T(4,128)}), f32[16,8,4,256]{3,2,0,1:T(4,128)S(1)}, u32[]{:S(2)}, u32[]{:S(2)}) async-start(f32[16,8,4,256]{3,2,0,1:T(4,128)} %copy.40), calls=%async_computation.1 | async-start | bytes 1048576 | tf_op jit(solution)/shard_map/all_to_all | solution.py:58
where the time goes:
time: 107 us; the launch traced here: 106 us
  blocking collectives  42 us (39%)
  waiting for transfers between devices  20.1 us (19%)
  local copies, waits for them, and re-layouts  17.5 us (16%)
  starting transfers between devices  14.1 us (13%)
  matrix products  5.34 us (5%)
  other arithmetic  3.86 us (4%)
  between operations  3.41 us (3%)
    unnamed x1, blocking collectives  42 us
    all_to_all x1, waiting for transfers between devices, shards(): lax.all_to_all(outgoing[0], 'gz', split_axis=2, concat_axis=2, tiled=True)  10.3 us
    dot_general x2, matrix products, accumulate(): jnp.dot(hits.astype(jnp.float32), values, precision=lax.Precision.HIGHEST...  5.34 us
    all_to_all x1, waiting for transfers between devices, shards(): lax.all_to_all(outgoing[1], 'gz', split_axis=2, concat_axis=2, tiled=True)  4.02 us
    all_to_all x1, starting transfers between devices, shards(): lax.all_to_all(outgoing[1], 'gz', split_axis=2, concat_axis=2, tiled=True)  3.6 us
    all_to_all x1, starting transfers between devices, shards(): lax.all_to_all(lax.all_to_all(outgoing[1], 'gz', split_axis=2, concat_axi...  3.56 us
    all_to_all x1, starting transfers between devices, shards(): lax.all_to_all(lax.all_to_all(outgoing[0], 'gz', split_axis=2, concat_axi...  3.49 us
    all_to_all x1, starting transfers between devices, shards(): lax.all_to_all(outgoing[0], 'gz', split_axis=2, concat_axis=2, tiled=True)  3.47 us
  transfers between devices with their start and end apart: 4, of which 4 were waited for; matrix products, arithmetic and copies ran while one was open for 12% of the time, Pallas kernels for 0%

commit v1 on v0

--- a/solution.py
+++ b/solution.py
@@ -56,7 +56,12 @@
     outgoing = (arrange(sums), arrange(fields))
     arrived = (
         lax.all_to_all(
-            lax.all_to_all(outgoing[0], "gz", split_axis=2, concat_axis=2, tiled=True),
+            jnp.concatenate(
+                lax.all_to_all(
+                    jnp.stack(jnp.split(outgoing[0], lax.axis_size("gz"), axis=2)), "gz", 0, 0
+                ),
+                axis=2,
+            ),
             ("gx", "gy"),
             split_axis=1,
             concat_axis=1,

time: 107 us -> 107 us (level)
    another operation x1 -> x3, local copies, waits for them, and re-layouts: 0.09 us -> 1.22 us  [the longest x2 1.14 us: shards(): jnp.stack(jnp.split(outgoing[0], lax.axis_size('gz'), axis=2))]
    all_to_all x2 -> x1, local copies, waits for them, and re-layouts: 1.18 us -> 0.04 us  [shards(): lax.all_to_all(jnp.concatenate(lax.all_to_all(jnp.stack(jnp.split(outgoin...]
    reshape x0 -> x1, local copies, waits for them, and re-layouts: none -> 1.14 us  [shards(): jnp.concatenate(lax.all_to_all(jnp.stack(jnp.split(outgoing[0], lax.axis_...]
    reshape x2 -> x1, local copies, waits for them, and re-layouts: 1.11 us -> 0.01 us  [arrange(): return rolled.reshape((slots, plane, line) + array.shape[1:])]
where the time goes in v1:
time: 107 us; the launch traced here: 106 us
  blocking collectives  41.9 us (39%)
  waiting for transfers between devices  20 us (19%)
  local copies, waits for them, and re-layouts  17.5 us (16%)
  starting transfers between devices  14.1 us (13%)
  matrix products  5.34 us (5%)
  other arithmetic  3.89 us (4%)
  between operations  3.43 us (3%)
    unnamed x1, blocking collectives  41.9 us
    all_to_all x1, waiting for transfers between devices, shards(): lax.all_to_all(jnp.stack(jnp.split(outgoing[0], lax.axis_size('gz'), axis...  10.3 us
    dot_general x2, matrix products, accumulate(): jnp.dot(hits.astype(jnp.float32), values, precision=lax.Precision.HIGHEST...  5.34 us
    all_to_all x1, waiting for transfers between devices, shards(): lax.all_to_all(outgoing[1], 'gz', split_axis=2, concat_axis=2, tiled=True)  3.93 us
    all_to_all x1, starting transfers between devices, shards(): lax.all_to_all(outgoing[1], 'gz', split_axis=2, concat_axis=2, tiled=True)  3.59 us
    all_to_all x1, starting transfers between devices, shards(): lax.all_to_all(lax.all_to_all(outgoing[1], 'gz', split_axis=2, concat_axi...  3.56 us
    all_to_all x1, starting transfers between devices, shards(): lax.all_to_all(jnp.concatenate(lax.all_to_all(jnp.stack(jnp.split(outgoin...  3.49 us
    all_to_all x1, starting transfers between devices, shards(): lax.all_to_all(jnp.stack(jnp.split(outgoing[0], lax.axis_size('gz'), axis...  3.47 us
  transfers between devices with their start and end apart: 4, of which 4 were waited for; matrix products, arithmetic and copies ran while one was open for 12% of the time, Pallas kernels for 0%

profile of v1, /device:TPU:0, one launch (start us, length us, event | category | flops | bytes accessed | tf_op | source)
XLA Modules:
  0.0 106.3 jit_solution(5674813857012857537)
XLA Ops:
  1.4 41.9 %all-reduce = s32[32]{0:T(128)S(1)} all-reduce(s32[32]{0:T(128)S(1)} %dynamic-update-slice), channel_id=1, replica_groups=mesh['gx'=4,'gy'=2,'gz'=4] {'gx','gy','gz'}, use_global_device_ids=true, to_apply=%add | all-reduce | flops 32 | bytes 256
  43.6 0.6 fusion.19
  44.3 0.6 dynamic_slice.25
  46.8 7.4 %while.16 = (s32[]{:T(128)}, f32[512,256]{1,0:T(8,128)S(1)}, s32[512]{0:T(512)S(1)}, s32[2048]{0:T(1024)}, f32[2048,256]{1,0:T(8,128)}, /*index=5*/s32[]{:T(128)}, s32[]{:T(128)}, s32[]{:T(128)}, s32[]{:T(128)}) while((s32[]{:T(128)}, f32[512,256]{1,0:T(8,128)S(1)}, s32[512]{0:T(512)S(1)}, s32[2048]{0:T(1024)}, ...), condition=%wide.region_3.4_spmd.clone, body=%wide.region_1.3_spmd.clone.sunk | while | flops 1612972544 | bytes 2121886 | solution.py:39
  46.9 0.7 dynamic_slice.55
  47.5 2.7 %fusion.24 = f32[512,256]{1,0:T(8,128)S(1)} fusion(f32[2048,256]{1,0:T(8,128)} %get-tuple-element.207, s32[]{:T(128)S(6)} %select_n.107, s32[1024]{0:T(1024)S(1)} %dynamic_slice.55, f32[512,256]{1,0:T(8,128)S(1)} %get-tuple-element.195, pred[]{:T(512)S(6)} %compare.20), kind=kOutput, calls=%fused_computation.8.clone.1 | convolution fusion | flops 1611399168 | bytes 2101253 | tf_op jit(solution)/shard_map/while/body/eval_jaxpr/dot_general | solution.py:30
  50.2 0.3 fusion.25
  50.5 0.7 dynamic_slice.55
  51.2 2.7 %fusion.24 = f32[512,256]{1,0:T(8,128)S(1)} fusion(f32[2048,256]{1,0:T(8,128)} %get-tuple-element.207, s32[]{:T(128)S(6)} %select_n.107, s32[1024]{0:T(1024)S(1)} %dynamic_slice.55, f32[512,256]{1,0:T(8,128)S(1)} %get-tuple-element.195, pred[]{:T(512)S(6)} %compare.20), kind=kOutput, calls=%fused_computation.8.clone.1 | convolution fusion | flops 1611399168 | bytes 2101253 | tf_op jit(solution)/shard_map/while/body/eval_jaxpr/dot_general | solution.py:30
  53.9 0.3 fusion.25
  54.3 0.5 broadcast.199
  54.8 0.7 reduce.5
  55.8 0.7 reshape.320
  56.4 3.6 %all-to-all-start.2 = ((f32[4,1,256]{2,1,0:T(1,128)}), f32[4,1,256]{2,1,0:T(1,128)S(1)}, u32[]{:S(2)}, u32[]{:S(2)}) async-start(f32[4,1,256]{2,1,0:T(1,128)} %reshape.320), calls=%async_computation.2 | async-start | bytes 8192 | tf_op jit(solution)/shard_map/all_to_all | solution.py:71
  60.2 0.3 copy.53
  60.6 1.1 %copy.57 = f32[4,16,8,1,256]{4,2,1,3,0:T(8,128)} copy(f32[4,16,8,1,256]{4,1,2,3,0:T(8,128)S(1)} %pad_maximum_fusion) | data formatting | bytes 1048576 | tf_op jit(solution)/shard_map/stack | solution.py:61
  61.7 3.9 %all-to-all-done.2 = f32[4,1,256]{2,1,0:T(1,128)S(1)} async-done(((f32[4,1,256]{2,1,0:T(1,128)}), f32[4,1,256]{2,1,0:T(1,128)S(1)}, u32[]{:S(2)}, u32[]{:S(2)}) %all-to-all-start.2) | async-done | bytes 4128 | tf_op jit(solution)/shard_map/all_to_all | solution.py:71
  65.6 3.5 %all-to-all-start = ((f32[4,16,8,1,256]{4,2,1,3,0:T(8,128)}), f32[4,16,8,1,256]{4,2,1,3,0:T(8,128)S(1)}, u32[]{:S(2)}, u32[]{:S(2)}) async-start(f32[4,16,8,1,256]{4,2,1,3,0:T(8,128)} %copy.57), calls=%async_computation | async-start | bytes 1048576 | tf_op jit(solution)/shard_map/all_to_all | solution.py:60
  69.3 0.5 broadcast.200
  69.8 0.7 reduce.6
  70.6 0.7 reshape.322
  71.3 10.3 %all-to-all-done = f32[4,16,8,1,256]{4,2,1,3,0:T(8,128)S(1)} async-done(((f32[4,16,8,1,256]{4,2,1,3,0:T(8,128)}), f32[4,16,8,1,256]{4,2,1,3,0:T(8,128)S(1)}, u32[]{:S(2)}, u32[]{:S(2)}) %all-to-all-start) | async-done | bytes 524320 | tf_op jit(solution)/shard_map/all_to_all | solution.py:60
  81.6 3.6 %all-to-all-start.3 = ((f32[8,1,128]{2,1,0:T(1,128)}), f32[8,1,128]{2,1,0:T(1,128)S(1)}, u32[]{:S(2)}, u32[]{:S(2)}) async-start(f32[8,1,128]{2,1,0:T(1,128)} %reshape.322), calls=%async_computation.3 | async-start | bytes 8192 | tf_op jit(solution)/shard_map/all_to_all | solution.py:70
  85.2 1.1 %copy.58 = f32[16,8,4,256]{3,2,0,1:T(4,128)} copy(f32[16,8,4,256]{3,1,0,2:T(8,128)S(1)} %bitcast.40) | data formatting | bytes 1048576 | tf_op jit(solution)/shard_map/reshape | solution.py:59
  86.4 3.5 %all-to-all-done.3 = f32[8,1,128]{2,1,0:T(1,128)S(1)} async-done(((f32[8,1,128]{2,1,0:T(1,128)}), f32[8,1,128]{2,1,0:T(1,128)S(1)}, u32[]{:S(2)}, u32[]{:S(2)}) %all-to-all-start.3) | async-done | bytes 4128 | tf_op jit(solution)/shard_map/all_to_all | solution.py:70
  89.8 3.5 %all-to-all-start.1 = ((f32[16,8,4,256]{3,2,0,1:T(4,128)}), f32[16,8,4,256]{3,2,0,1:T(4,128)S(1)}, u32[]{:S(2)}, u32[]{:S(2)}) async-start(f32[16,8,4,256]{3,2,0,1:T(4,128)} %copy.58), calls=%async_computation.1 | async-start | bytes 1048576 | tf_op jit(solution)/shard_map/all_to_all | solution.py:58
  93.7 0.7 reduce.7
  94.8 3.0 %scatter_custom_fusion.1 = s32[512]{0:T(512)} fusion(s32[512]{0:T(512)S(1)} %bitcast.48, s32[512]{0:T(512)S(1)} %bitcast.52, s32[]{:T(128)} %constant.107.clone.1), kind=kCustom, calls=%fused_computation.45 | custom fusion | bytes 2052 | tf_op jit(solution)/shard_map/scatter | solution.py:95
  97.8 3.0 %scatter_custom_fusion.2 = s32[512]{0:T(512)} fusion(s32[512]{0:T(512)S(1)} %bitcast.49, s32[512]{0:T(512)S(1)} %bitcast.51, s32[]{:T(128)} %constant.111.clone.1), kind=kCustom, calls=%fused_computation.43 | custom fusion | bytes 2052 | tf_op jit(solution)/shard_map/scatter | solution.py:100
  100.8 2.2 %all-to-all-done.1 = f32[16,8,4,256]{3,2,0,1:T(4,128)S(1)} async-done(((f32[16,8,4,256]{3,2,0,1:T(4,128)}), f32[16,8,4,256]{3,2,0,1:T(4,128)S(1)}, u32[]{:S(2)}, u32[]{:S(2)}) %all-to-all-start.1) | async-done | bytes 524320 | tf_op jit(solution)/shard_map/all_to_all | solution.py:58
  103.0 0.2 reshape.279
  103.2 3.0 %scatter_custom_fusion = f32[512,256]{1,0:T(8,128)} fusion(s32[512]{0:T(512)S(1)} %bitcast.50, f32[512,256]{1,0:T(8,128)S(1)} %reshape.279, f32[]{:T(128)} %constant.100.clone.1), kind=kCustom, calls=%fused_computation.17 | custom fusion | bytes 524292 | tf_op jit(solution)/shard_map/scatter | solution.py:90
  (38 shorter events, 2.1 us)
Async XLA Ops:
  46.8 8.0 %copy-start = (s32[1,512]{1,0:T(1,128)S(1)}, s32[1,512]{1,0:T(1,128)}, u32[]{:S(2)}) copy-start(s32[1,512]{1,0:T(1,128)} %param.8) | copy-start | bytes 6148
  56.4 9.2 %all-to-all-start.2 = ((f32[4,1,256]{2,1,0:T(1,128)}), f32[4,1,256]{2,1,0:T(1,128)S(1)}, u32[]{:S(2)}, u32[]{:S(2)}) async-start(f32[4,1,256]{2,1,0:T(1,128)} %reshape.320), calls=%async_computation.2 | async-start | bytes 8192 | tf_op jit(solution)/shard_map/all_to_all | solution.py:71
  65.6 16.0 %all-to-all-start = ((f32[4,16,8,1,256]{4,2,1,3,0:T(8,128)}), f32[4,16,8,1,256]{4,2,1,3,0:T(8,128)S(1)}, u32[]{:S(2)}, u32[]{:S(2)}) async-start(f32[4,16,8,1,256]{4,2,1,3,0:T(8,128)} %copy.57), calls=%async_computation | async-start | bytes 1048576 | tf_op jit(solution)/shard_map/all_to_all | solution.py:60
  81.6 8.2 %all-to-all-start.3 = ((f32[8,1,128]{2,1,0:T(1,128)}), f32[8,1,128]{2,1,0:T(1,128)S(1)}, u32[]{:S(2)}, u32[]{:S(2)}) async-start(f32[8,1,128]{2,1,0:T(1,128)} %reshape.322), calls=%async_computation.3 | async-start | bytes 8192 | tf_op jit(solution)/shard_map/all_to_all | solution.py:70
  89.8 13.2 %all-to-all-start.1 = ((f32[16,8,4,256]{3,2,0,1:T(4,128)}), f32[16,8,4,256]{3,2,0,1:T(4,128)S(1)}, u32[]{:S(2)}, u32[]{:S(2)}) async-start(f32[16,8,4,256]{3,2,0,1:T(4,128)} %copy.58), calls=%async_computation.1 | async-start | bytes 1048576 | tf_op jit(solution)/shard_map/all_to_all | solution.py:58
